TPU v7x, 32 devices: a whole 2x2x4 slice. The times are simulated.
32 devices in a mesh: groups: 2 (over y), tm: 4 (over z), chan: 4 (over x, core).
Axes of the slice: x: 2, y: 2, z: 4, core: 2. Of those that a mesh axis runs over, the one named last changes fastest.
Arguments:
- tokens: bfloat16 [1024, 4096], P(('groups', 'tm'), 'chan'), parts along dimension 0, may hold values from -6 to 6
- in_weight: bfloat16 [4096, 8192], P('chan'), may hold values from -0.125 to 0.125
- recur_weight: float32 [2048, 2], P('chan'), may hold values from -0.75 to 0.75
- gate_bias: float32 [2048, 4], P('chan'), may hold values from -2 to 13
- forget_offset: float32 [1024], P(('groups', 'tm')), parts along dimension 0, may hold values from 0 to 14
Outputs:
- hidden_states: float32 [2048, 1024], P('chan', ('groups', 'tm')), parts along dimension 1
There are 2 independent parts, one for each index of `groups`. A program takes and returns all parts, laid end to end along the dimension named above; an argument that names none is the same for every part. Nothing has to cross between parts.
All inputs are finite; a program needn't handle non-finite values.
Results may differ from a plain program's by a relative error of at most 0.0003.
Values may be sent and summed in bfloat16 or wider, within the bound.
A program may use at most 128 MiB of HBM per device.

v0:
```python
import functools

import jax
import jax.numpy as jnp
from jax import lax
from jax.experimental import pallas as pl
from jax.experimental.pallas import tpu as pltpu
from jax.sharding import PartitionSpec as P

MESH = pl.DeviceIdType.MESH
LANES = 128
SUB = 8
GATES = 4
AHEAD = 4
WIRE = jnp.float32


def compose(early, later):
    e_one, e_two, e_three, e_four, e_five, e_six = early
    l_one, l_two, l_three, l_four, l_five, l_six = later
    return (
        l_one * e_one + l_two * e_three,
        l_one * e_two + l_two * e_four,
        l_three * e_one + l_four * e_three,
        l_three * e_two + l_four * e_four,
        l_one * e_five + l_two * e_six + l_five,
        l_three * e_five + l_four * e_six + l_six,
    )


def compose_lower(early, later):
    e_one, e_three, e_four, e_five, e_six = early
    l_one, l_three, l_four, l_five, l_six = later
    return (
        l_one * e_one,
        l_three * e_one + l_four * e_three,
        l_four * e_four,
        l_one * e_five + l_five,
        l_three * e_five + l_four * e_six + l_six,
    )


def kernel(
    chips, blocks, tm,
    tokens_hbm, weight_hbm, recur_ref, bias_ref, offset_ref, out_ref,
    tokens_v, weight_v, own_v, give_v, take_v, far_out, far_in,
    turned, pre_v, input_v, recur_v, prefix_v, edge_v, maps_v, hidden_v,
    tokens_sem, weight_sem, give_send, give_recv, far_send, far_recv, map_send, map_recv,
):
    my_chan = lax.axis_index("chan")
    my_tm = lax.axis_index("tm")
    chip = my_chan // 2
    core = my_chan % 2
    partner = chip * 2 + (1 - core)
    units = chips * blocks
    width = GATES * LANES
    steps = tokens_v.shape[0]
    run = steps // SUB

    def chip_of(rank):
        return lax.rem(chip + rank + 1, chips)

    def weight_copy(index):
        unit = index // 2
        mine = index % 2
        target = chip_of(unit // blocks) * 2 + jnp.where(mine == 1, core, 1 - core)
        column = pl.multiple_of((target * blocks + unit % blocks) * width, width)
        return pltpu.make_async_copy(
            weight_hbm.at[:, pl.ds(column, width)], weight_v.at[index], weight_sem.at[index]
        )

    def give_copy(unit):
        return pltpu.make_async_remote_copy(
            src_ref=give_v.at[unit],
            dst_ref=take_v.at[unit],
            send_sem=give_send.at[unit],
            recv_sem=give_recv.at[unit],
            device_id={"chan": partner},
            device_id_type=MESH,
        )

    def far_copy(unit):
        return pltpu.make_async_remote_copy(
            src_ref=far_out.at[unit],
            dst_ref=far_in.at[unit],
            send_sem=far_send.at[unit],
            recv_sem=far_recv.at[unit],
            device_id={"chan": chip_of(unit // blocks) * 2 + core},
            device_id_type=MESH,
        )

    def map_copy(turn, block, hop):
        peer = lax.rem(my_tm + hop, tm)
        slot = (turn * blocks + block) * tm + my_tm
        sem = (turn * blocks + block) * tm + hop
        return pltpu.make_async_remote_copy(
            src_ref=maps_v.at[slot],
            dst_ref=maps_v.at[slot],
            send_sem=map_send.at[sem],
            recv_sem=map_recv.at[sem],
            device_id={"tm": peer},
            device_id_type=MESH,
        )

    tokens_copy = pltpu.make_async_copy(tokens_hbm, tokens_v, tokens_sem)
    tokens_copy.start()
    for index in range(AHEAD):
        weight_copy(index).start()

    barrier = pltpu.get_barrier_semaphore()
    pl.semaphore_signal(barrier, inc=1, device_id={"chan": partner}, device_id_type=MESH)
    for rank in range(chips - 1):
        pl.semaphore_signal(
            barrier, inc=1, device_id={"chan": chip_of(rank) * 2 + core}, device_id_type=MESH
        )
    for hop in range(1, tm):
        pl.semaphore_signal(
            barrier, inc=1, device_id={"tm": lax.rem(my_tm + hop, tm)}, device_id_type=MESH
        )

    for block in range(blocks):
        rows = slice(block * LANES, (block + 1) * LANES)
        for which in range(2):
            wide = jnp.broadcast_to(recur_ref[rows, which : which + 1], (LANES, LANES))
            recur_v[block, which] = wide.T[0:SUB]

    tokens_copy.wait()
    pl.semaphore_wait(barrier, chips + tm - 1)

    def product(index):
        weight_copy(index).wait()

        @pl.when(index + AHEAD < 2 * units)
        def _():
            weight_copy(index + AHEAD).start()

        return jnp.dot(tokens_v[...], weight_v[index], preferred_element_type=jnp.float32)

    def forward(unit):
        give_copy(unit).wait_recv()
        far_out[unit] = (own_v[unit] + take_v[unit]).astype(far_out.dtype)
        far_copy(unit).start()

    def matmul_step(unit, carry):
        give_v[unit] = product(2 * unit)
        give_copy(unit).start()
        own_v[unit] = product(2 * unit + 1)

        @pl.when((unit >= 1) & (unit <= units - blocks))
        def _():
            forward(unit - 1)

        return carry

    lax.fori_loop(0, units, matmul_step, 0)

    row_id = lax.broadcasted_iota(jnp.int32, (SUB, LANES), 0)

    def at(step):
        return pl.ds(step, SUB, stride=run)

    def shifted(parts, by, identity):
        return tuple(
            jnp.where(row_id < by, unit_value, pltpu.roll(part, by, 0))
            for part, unit_value in zip(parts, identity)
        )

    lower_identity = (1.0, 0.0, 1.0, 0.0, 0.0)
    identity = (1.0, 0.0, 0.0, 1.0, 0.0, 0.0)

    def publish(turn, block, total, fold, neutral):
        for by in (1, 2, 4):
            total = fold(shifted(total, by, neutral), total)
        if len(total) == 5:
            total = (total[0], jnp.zeros_like(total[0])) + tuple(total[1:])
        slot = (turn * blocks + block) * tm + my_tm
        before = shifted(total, 1, identity)
        for row in range(6):
            edge_v[turn, block, row] = before[row]
            maps_v[slot, row : row + 1, :] = total[row][SUB - 1 : SUB]
        maps_v[slot, 6:8, :] = jnp.zeros((2, LANES), jnp.float32)
        for hop in range(1, tm):
            map_copy(turn, block, hop).start()

    def arriving(turn, block):
        for hop in range(1, tm):
            map_copy(turn, block, hop).wait_recv()
        cell = jnp.zeros((1, LANES), jnp.float32)
        hidden = jnp.zeros((1, LANES), jnp.float32)
        for source in range(tm - 1):
            held = maps_v[(turn * blocks + block) * tm + source]
            ahead = source < my_tm
            cell, hidden = (
                jnp.where(ahead, held[0:1] * cell + held[1:2] * hidden + held[4:5], cell),
                jnp.where(ahead, held[2:3] * cell + held[3:4] * hidden + held[5:6], hidden),
            )
        edge = [edge_v[turn, block, row] for row in range(6)]
        return (
            edge[0] * cell + edge[1] * hidden + edge[4],
            edge[2] * cell + edge[3] * hidden + edge[5],
        )

    def first(block):
        unit = (chips - 1) * blocks + block
        give_copy(unit).wait_recv()
        total = own_v[unit] + take_v[unit]
        for rank in range(chips - 1):
            far_copy(rank * blocks + block).wait_recv()
            total = total + far_in[rank * blocks + block].astype(jnp.float32)
        for piece in range(GATES):
            lanes = slice(piece * LANES, (piece + 1) * LANES)
            turned[lanes, :] = total[:, lanes].T
        rows = pl.ds(pl.multiple_of(block * LANES, LANES), LANES)
        biases = bias_ref[rows, :]
        for gate in range(GATES):
            value = turned[pl.ds(gate, LANES, stride=GATES), :] + biases[:, gate : gate + 1]
            if gate == 1:
                value = value - offset_ref[...]
            pre_v[block, gate] = value.T
        recur_out = recur_v[block, 1]
        prefix = None
        for step in range(run):
            input_gate = jax.nn.sigmoid(pre_v[block, 0, at(step), :])
            forget = jax.nn.sigmoid(pre_v[block, 1, at(step), :])
            cand = jnp.tanh(pre_v[block, 2, at(step), :])
            output = jax.nn.sigmoid(pre_v[block, 3, at(step), :])
            fresh = input_gate * cand
            squashed = jnp.tanh(fresh)
            slope = 1.0 - squashed * squashed
            input_v[block, step] = fresh
            term = (
                forget,
                output * slope * forget,
                output * (1.0 - output) * recur_out * squashed,
                fresh,
                output * squashed,
            )
            prefix = term if prefix is None else compose_lower(prefix, term)
            for row, part in enumerate(prefix):
                prefix_v[block, row, step] = part
        publish(0, block, prefix, compose_lower, lower_identity)

    def jacobian(block, step, cell, hidden, recur_forget, recur_out):
        forget = jax.nn.sigmoid(pre_v[block, 1, at(step), :] + recur_forget * hidden)
        output = jax.nn.sigmoid(pre_v[block, 3, at(step), :] + recur_out * hidden)
        fresh = input_v[block, step]
        squashed = jnp.tanh(forget * cell + fresh)
        slope = output * (1.0 - squashed * squashed)
        cell_hidden = cell * forget * (1.0 - forget) * recur_forget
        hidden_cell = slope * forget
        hidden_hidden = output * (1.0 - output) * recur_out * squashed + slope * cell_hidden
        return (
            forget,
            cell_hidden,
            hidden_cell,
            hidden_hidden,
            fresh - cell_hidden * hidden,
            output * squashed - hidden_cell * cell - hidden_hidden * hidden,
        )

    def second(block):
        start_cell, start_hidden = arriving(0, block)
        recur_forget, recur_out = recur_v[block, 0], recur_v[block, 1]
        cell, hidden = start_cell, start_hidden
        prefix = None
        for step in range(run):
            term = jacobian(block, step, cell, hidden, recur_forget, recur_out)
            if step + 1 < run:
                past = [prefix_v[block, row, step] for row in range(5)]
                cell = past[0] * start_cell + past[3]
                hidden = past[1] * start_cell + past[2] * start_hidden + past[4]
            prefix = term if prefix is None else compose(prefix, term)
            for row, part in ((0, prefix[2]), (1, prefix[3]), (2, prefix[5])):
                prefix_v[block, row + 5, step] = part
        publish(1, block, prefix, compose, identity)

    def third(block):
        start_cell, start_hidden = arriving(1, block)
        for step in range(run):
            past = [prefix_v[block, row + 5, step] for row in range(3)]
            hidden_v[at(step), :] = past[0] * start_cell + past[1] * start_hidden + past[2]
        rows = pl.ds(pl.multiple_of(block * LANES, LANES), LANES)
        out_ref[rows, :] = hidden_v[...].T

    def scan_step(turn, carry):
        @pl.when(turn < blocks)
        def _():
            first(turn)

        @pl.when((turn >= 1) & (turn <= blocks))
        def _():
            second(turn - 1)

        @pl.when(turn >= 2)
        def _():
            third(turn - 2)

        return carry

    lax.fori_loop(0, blocks + 2, scan_step, 0)

    def settle_units(unit, carry):
        give_copy(unit).wait_send()

        @pl.when(unit < units - blocks)
        def _():
            far_copy(unit).wait_send()

        return carry

    lax.fori_loop(0, units, settle_units, 0)

    def settle_maps(index, carry):
        for hop in range(1, tm):
            map_copy(index // blocks, index % blocks, hop).wait_send()
        return carry

    lax.fori_loop(0, 2 * blocks, settle_maps, 0)


def shards(chan, tm, tokens, in_weight, recur_weight, gate_bias, forget_offset):
    steps, depth = tokens.shape
    channels = recur_weight.shape[0]
    chips = chan // 2
    blocks = channels // LANES
    units = chips * blocks
    far = max(1, units - blocks)
    width = GATES * LANES
    run = steps // SUB
    vmem = pl.BlockSpec(memory_space=pltpu.VMEM)
    hbm = pl.BlockSpec(memory_space=pl.ANY)
    dma = pltpu.SemaphoreType.DMA
    float32 = jnp.float32
    return pl.pallas_call(
        functools.partial(kernel, chips, blocks, tm),
        out_shape=jax.ShapeDtypeStruct((channels, steps), float32),
        in_specs=[hbm, hbm, vmem, vmem, vmem],
        out_specs=vmem,
        scratch_shapes=[
            pltpu.VMEM((steps, depth), tokens.dtype),
            pltpu.VMEM((2 * units, depth, width), in_weight.dtype),
            pltpu.VMEM((units, steps, width), float32),
            pltpu.VMEM((units, steps, width), float32),
            pltpu.VMEM((units, steps, width), float32),
            pltpu.VMEM((far, steps, width), WIRE),
            pltpu.VMEM((far, steps, width), WIRE),
            pltpu.VMEM((width, steps), float32),
            pltpu.VMEM((blocks, GATES, steps, LANES), float32),
            pltpu.VMEM((blocks, run, SUB, LANES), float32),
            pltpu.VMEM((blocks, 2, SUB, LANES), float32),
            pltpu.VMEM((blocks, 8, run, SUB, LANES), float32),
            pltpu.VMEM((2, blocks, 6, SUB, LANES), float32),
            pltpu.VMEM((2 * blocks * tm, SUB, LANES), float32),
            pltpu.VMEM((steps, LANES), float32),
            dma,
            dma((2 * units,)),
            dma((units,)),
            dma((units,)),
            dma((far,)),
            dma((far,)),
            dma((2 * blocks * tm,)),
            dma((2 * blocks * tm,)),
        ],
        compiler_params=pltpu.CompilerParams(
            collective_id=0, has_side_effects=True, vmem_limit_bytes=63000 * 1024
        ),
    )(tokens, in_weight, recur_weight, gate_bias, forget_offset.reshape(1, steps))


def solution(mesh):
    placed = (
        P(("groups", "tm"), "chan"),
        P("chan", None),
        P("chan", None),
        P("chan", None),
        P(("groups", "tm")),
    )
    return jax.shard_map(
        functools.partial(shards, mesh.shape["chan"], mesh.shape["tm"]),
        mesh=mesh,
        in_specs=placed,
        out_specs=P("chan", ("groups", "tm")),
        check_vma=False,
    )
```

profile of v0, /device:TPU:0, one launch (start us, length us, event | category | flops | bytes accessed | tf_op | source)
XLA Modules:
  0.0 47.3 jit_solution(8881030857972640576)
XLA Ops:
  0.0 1.5 %copy.6.recur_ref = f32[512,2]{1,0:T(8,128)} copy(f32[512,2]{0,1:T(2,128)} %param.7) | data formatting | bytes 8192 | tf_op args[2]
  1.5 1.5 %copy.7.bias_ref = f32[512,4]{1,0:T(8,128)} copy(f32[512,4]{0,1:T(4,128)} %param.8) | data formatting | bytes 16384 | tf_op args[3]
  3.1 42.5 %shard_map.55 = f32[512,128]{1,0:T(8,128)} custom-call(bf16[128,1024]{1,0:T(8,128)(2,1)} %tokens_hbm.1, bf16[1024,8192]{1,0:T(8,128)(2,1)} %weight_hbm.1, f32[512,2]{1,0:T(8,128)} %copy.6.recur_ref, f32[512,4]{1,0:T(8,128)} %copy.7.bias_ref, f32[1,128]{1,0:T(1,128)} %bitcast.1), custom_call_target="tpu_custom_call" | custom-call | tf_op jit(solution)/shard_map/pallas_call | solution.py:334
  45.6 1.7 %copy.9 = f32[512,128]{1,0:T(8,128)} copy(f32[512,128]{1,0:T(8,128)} %shard_map.55) | data formatting | bytes 524288
where the time goes:
time: 47.5 us; the launch traced here: 47.3 us
  Pallas kernels  42.5 us (89%)
  local copies, waits for them, and re-layouts  4.75 us (10%)
    pallas_call x1, Pallas kernels, shards(): pl.pallas_call(functools.partial(kernel, chips, blocks, tm), out_shape=ja...  42.5 us
    unnamed x3, local copies, waits for them, and re-layouts  4.75 us

commit v1 on v0

v1 whole, which is shorter than its diff:
```python
import functools
import math

import jax
import jax.numpy as jnp
from jax import lax
from jax.experimental import pallas as pl
from jax.experimental.pallas import tpu as pltpu
from jax.sharding import PartitionSpec as P

MESH = pl.DeviceIdType.MESH
LANES = 128
SUB = 8
GATES = 4
AHEAD = 6
PIECES = 2
LAG = 3
TOKEN_MOST = 6.0
WEIGHT_MOST = 0.125
KNEE = 8.0
SLOPE = 25.5
OCTAVES = 252.0
FLOOR = 126.0


def compose(early, later):
    e_one, e_two, e_three, e_four, e_five, e_six = early
    l_one, l_two, l_three, l_four, l_five, l_six = later
    return (
        l_one * e_one + l_two * e_three,
        l_one * e_two + l_two * e_four,
        l_three * e_one + l_four * e_three,
        l_three * e_two + l_four * e_four,
        l_one * e_five + l_two * e_six + l_five,
        l_three * e_five + l_four * e_six + l_six,
    )


def compose_lower(early, later):
    e_one, e_three, e_four, e_five, e_six = early
    l_one, l_three, l_four, l_five, l_six = later
    return (
        l_one * e_one,
        l_three * e_one + l_four * e_three,
        l_four * e_four,
        l_one * e_five + l_five,
        l_three * e_five + l_four * e_six + l_six,
    )


def sigmoid(value):
    return 0.5 * jnp.tanh(0.5 * value) + 0.5


def knee_rate(most):
    return (OCTAVES - SLOPE * KNEE) / math.log(most / KNEE)


def encode(value, most):
    rate = knee_rate(most)
    size = jnp.abs(value)
    beyond = rate * jnp.log(jnp.maximum(size, KNEE)) + (SLOPE * KNEE - rate * math.log(KNEE))
    power = jnp.exp2(jnp.minimum(SLOPE * size, beyond) - FLOOR)
    return jnp.where(value < 0.0, -power, power).astype(jnp.bfloat16)


def decode(code, most):
    rate = knee_rate(most)
    level = jnp.log2(jnp.abs(code)) + FLOOR
    beyond = KNEE * jnp.exp((jnp.maximum(level, SLOPE * KNEE) - SLOPE * KNEE) * (1.0 / rate))
    size = jnp.where(level <= SLOPE * KNEE, level * (1.0 / SLOPE), beyond)
    return jnp.where(code < 0.0, -size, size)


def kernel(
    chips, blocks, tm, most,
    tokens_hbm, weight_hbm, recur_hbm, bias_hbm, offset_hbm, out_ref,
    tokens_v, sorted_v, weight_v, recur_v, bias_v, offset_v,
    part_v, take_v, far_out, far_in, unmix, code_v,
    turned, near_v, pre_v, input_v, prefix_v, edge_v, maps_v, hidden_v,
    tokens_sem, small_sem, weight_sem, give_send, give_recv, far_send, far_recv, map_send, map_recv,
    ready_sem,
):
    my_chan = lax.axis_index("chan")
    my_tm = lax.axis_index("tm")
    chip = my_chan // 2
    core = my_chan % 2
    partner = chip * 2 + (1 - core)
    held = blocks * PIECES
    units = chips * held
    far = units - held
    width = GATES * LANES
    thin = width // PIECES
    steps = tokens_v.shape[0]
    run = steps // SUB

    def chip_of(rank):
        return lax.rem(chip + rank + 1, chips)

    def place(index):
        near = jnp.where(index >= 2 * far, 1, 0)
        local = index - near * 2 * far
        count = jnp.where(near == 1, held, far)
        late = jnp.where(local >= count, 1, 0)
        return late, near * far + local - late * count

    def weight_copy(index):
        owner, unit = place(index)
        target = chip_of(unit // held) * 2 + owner
        column = pl.multiple_of((target * held + unit % held) * thin, thin)
        return pltpu.make_async_copy(
            weight_hbm.at[:, pl.ds(column, thin)], weight_v.at[index], weight_sem.at[index]
        )

    def give_copy(unit):
        return pltpu.make_async_remote_copy(
            src_ref=part_v.at[unit, 1 - core],
            dst_ref=take_v.at[unit],
            send_sem=give_send.at[unit],
            recv_sem=give_recv.at[unit],
            device_id={"chan": partner},
            device_id_type=MESH,
        )

    def far_copy(unit):
        return pltpu.make_async_remote_copy(
            src_ref=far_out.at[unit],
            dst_ref=far_in.at[unit],
            send_sem=far_send.at[unit],
            recv_sem=far_recv.at[unit],
            device_id={"chan": chip_of(unit // held) * 2 + core},
            device_id_type=MESH,
        )

    def map_copy(turn, block, source, target):
        slot = (turn * blocks + block) * tm + source
        return pltpu.make_async_remote_copy(
            src_ref=maps_v.at[slot],
            dst_ref=maps_v.at[slot],
            send_sem=map_send.at[(turn * blocks + block) * tm + target],
            recv_sem=map_recv.at[slot],
            device_id={"tm": target},
            device_id_type=MESH,
        )

    tokens_copy = pltpu.make_async_copy(tokens_hbm, tokens_v, tokens_sem)
    tokens_copy.start()
    for index in range(AHEAD):
        weight_copy(index).start()

    barrier = pltpu.get_barrier_semaphore()
    pl.semaphore_signal(barrier, inc=1, device_id={"chan": partner}, device_id_type=MESH)
    for rank in range(chips - 1):
        pl.semaphore_signal(
            barrier, inc=1, device_id={"chan": chip_of(rank) * 2 + core}, device_id_type=MESH
        )

    def greet(peer, carry):
        pl.semaphore_signal(barrier, inc=1, device_id={"tm": peer}, device_id_type=MESH)
        return carry

    lax.fori_loop(my_tm + 1, tm, greet, 0)

    small = [
        pltpu.make_async_copy(held, local, small_sem.at[index])
        for index, (held, local) in enumerate(
            ((recur_hbm, recur_v), (bias_hbm, bias_v), (offset_hbm, offset_v))
        )
    ]
    for copy in small:
        copy.start()

    row = lax.broadcasted_iota(jnp.int32, (steps, steps), 0)
    column = lax.broadcasted_iota(jnp.int32, (steps, steps), 1)
    sort = jnp.where(column == (row % SUB) * run + row // SUB, 1.0, 0.0).astype(tokens_v.dtype)
    row = lax.broadcasted_iota(jnp.int32, (width, width), 0)
    column = lax.broadcasted_iota(jnp.int32, (width, width), 1)
    wanted = (column % LANES) * GATES + column // LANES
    unmix[...] = jnp.where(row == wanted, 1.0, 0.0).astype(jnp.bfloat16)

    tokens_copy.wait()
    sorted_v[...] = jnp.dot(sort, tokens_v[...], preferred_element_type=jnp.float32).astype(
        sorted_v.dtype
    )
    pl.semaphore_wait(barrier, chips + my_tm)

    def answer(peer, carry):
        pl.semaphore_signal(ready_sem, inc=1, device_id={"tm": peer}, device_id_type=MESH)
        return carry

    lax.fori_loop(0, my_tm, answer, 0)

    def product(index):
        weight_copy(index).wait()

        @pl.when(index + AHEAD < 2 * units)
        def _():
            weight_copy(index + AHEAD).start()

        return jnp.dot(sorted_v[...], weight_v[index], preferred_element_type=jnp.float32)

    def forward(unit):
        give_copy(unit).wait_recv()
        far_out[unit] = encode(part_v[unit, core] + take_v[unit], most)
        far_copy(unit).start()

    def matmul_step(index, carry):
        owner, unit = place(index)
        part_v[unit, owner] = product(index)

        @pl.when(owner != core)
        def _():
            give_copy(unit).start()

        sent = index - core * far - LAG

        @pl.when((sent >= 0) & (sent < far))
        def _():
            forward(sent)

        return carry

    lax.fori_loop(0, 2 * units, matmul_step, 0)

    for copy in small:
        copy.wait()

    def near(block, carry):
        for piece in range(PIECES):
            unit = far + block * PIECES + piece
            give_copy(unit).wait_recv()
            total = part_v[unit, core] + take_v[unit]
            for tile in range(thin // LANES):
                lanes = slice(tile * LANES, (tile + 1) * LANES)
                turned[piece * thin + tile * LANES : piece * thin + (tile + 1) * LANES, :] = total[:, lanes].T
        rows = pl.ds(pl.multiple_of(block * LANES, LANES), LANES)
        for gate in range(GATES):
            value = turned[pl.ds(gate, LANES, stride=GATES), :].T
            near_v[block, gate] = value + bias_v[gate : gate + 1, rows]
        return carry

    lax.fori_loop(0, blocks, near, 0)
    wide = jnp.broadcast_to(offset_v[...], (LANES, steps)).T
    for step in range(run):
        hidden_v[step * SUB : (step + 1) * SUB] = wide[step * SUB : (step + 1) * SUB]
    for step in range(run):
        late = hidden_v[pl.ds(step, SUB, stride=run), :]
        for block in range(blocks):
            rows = slice(step * SUB, (step + 1) * SUB)
            near_v[block, 1, rows] = near_v[block, 1, rows] - late

    row_id = lax.broadcasted_iota(jnp.int32, (SUB, LANES), 0)

    def at(step):
        return slice(step * SUB, (step + 1) * SUB)

    def recur_rows(block):
        rows = pl.ds(pl.multiple_of(block * LANES, LANES), LANES)
        return [
            jnp.broadcast_to(recur_v[which : which + 1, rows], (SUB, LANES)) for which in range(2)
        ]

    def shifted(parts, by, identity):
        return tuple(
            jnp.where(row_id < by, unit_value, pltpu.roll(part, by, 0))
            for part, unit_value in zip(parts, identity)
        )

    lower_identity = (1.0, 0.0, 1.0, 0.0, 0.0)
    identity = (1.0, 0.0, 0.0, 1.0, 0.0, 0.0)

    def publish(turn, block, total, fold, neutral):
        for by in (1, 2, 4):
            total = fold(shifted(total, by, neutral), total)
        if len(total) == 5:
            total = (total[0], jnp.zeros_like(total[0])) + tuple(total[1:])
        slot = (turn * blocks + block) * tm + my_tm
        for part in range(6):
            maps_v[slot, part : part + 1, :] = total[part][SUB - 1 : SUB]
        maps_v[slot, 6:8, :] = jnp.zeros((2, LANES), jnp.float32)

        def send(back, carry):
            map_copy(turn, block, my_tm, tm - 1 - back).start()
            return carry

        lax.fori_loop(0, tm - 1 - my_tm, send, 0)
        before = shifted(total, 1, identity)
        for part in range(6):
            edge_v[turn, block, part] = before[part]

    def arriving(turn, block):
        def take(source, state):
            cell, hidden = state
            map_copy(turn, block, source, my_tm).wait_recv()
            held = maps_v[(turn * blocks + block) * tm + source]
            return (
                held[0:1] * cell + held[1:2] * hidden + held[4:5],
                held[2:3] * cell + held[3:4] * hidden + held[5:6],
            )

        zero = jnp.zeros((1, LANES), jnp.float32)
        cell, hidden = lax.fori_loop(0, my_tm, take, (zero, zero))
        edge = [edge_v[turn, block, part] for part in range(6)]
        return (
            edge[0] * cell + edge[1] * hidden + edge[4],
            edge[2] * cell + edge[3] * hidden + edge[5],
        )

    def first(block):
        for rank in range(chips - 1):
            code = jnp.zeros((steps, width), jnp.float32)
            for piece in range(PIECES):
                unit = rank * held + block * PIECES + piece
                far_copy(unit).wait_recv()
                code = code + jnp.dot(
                    far_in[unit],
                    unmix[piece * thin : (piece + 1) * thin, :],
                    preferred_element_type=jnp.float32,
                )
            for gate in range(GATES):
                code_v[rank, gate] = code[:, gate * LANES : (gate + 1) * LANES]
        _, recur_out = recur_rows(block)
        prefix = None
        for step in range(run):
            total = [near_v[block, gate, at(step)] for gate in range(GATES)]
            for rank in range(chips - 1):
                total = [
                    value + decode(code_v[rank, gate, at(step)], most)
                    for gate, value in enumerate(total)
                ]
            pre_v[block, 0, step] = total[1]
            pre_v[block, 1, step] = total[3]
            forget = sigmoid(total[1])
            output = sigmoid(total[3])
            fresh = sigmoid(total[0]) * jnp.tanh(total[2])
            squashed = jnp.tanh(fresh)
            slope = 1.0 - squashed * squashed
            input_v[block, step] = fresh
            term = (
                forget,
                output * slope * forget,
                output * (1.0 - output) * recur_out * squashed,
                fresh,
                output * squashed,
            )
            prefix = term if prefix is None else compose_lower(prefix, term)
            for part, value in enumerate(prefix):
                prefix_v[block, part, step] = value
        publish(0, block, prefix, compose_lower, lower_identity)

    def jacobian(block, step, cell, hidden, recur_forget, recur_out):
        forget = sigmoid(pre_v[block, 0, step] + recur_forget * hidden)
        output = sigmoid(pre_v[block, 1, step] + recur_out * hidden)
        fresh = input_v[block, step]
        squashed = jnp.tanh(forget * cell + fresh)
        slope = output * (1.0 - squashed * squashed)
        cell_hidden = cell * forget * (1.0 - forget) * recur_forget
        hidden_cell = slope * forget
        hidden_hidden = output * (1.0 - output) * recur_out * squashed + slope * cell_hidden
        return (
            forget,
            cell_hidden,
            hidden_cell,
            hidden_hidden,
            fresh - cell_hidden * hidden,
            output * squashed - hidden_cell * cell - hidden_hidden * hidden,
        )

    def second(block):
        start_cell, start_hidden = arriving(0, block)
        recur_forget, recur_out = recur_rows(block)
        cell, hidden = start_cell, start_hidden
        prefix = None
        for step in range(run):
            term = jacobian(block, step, cell, hidden, recur_forget, recur_out)
            if step + 1 < run:
                past = [prefix_v[block, part, step] for part in range(5)]
                cell = past[0] * start_cell + past[3]
                hidden = past[1] * start_cell + past[2] * start_hidden + past[4]
            prefix = term if prefix is None else compose(prefix, term)
            for part, value in ((0, prefix[2]), (1, prefix[3]), (2, prefix[5])):
                prefix_v[block, part + 5, step] = value
        publish(1, block, prefix, compose, identity)

    def third(block):
        start_cell, start_hidden = arriving(1, block)
        for step in range(run):
            past = [prefix_v[block, part + 5, step] for part in range(3)]
            hidden_v[pl.ds(step, SUB, stride=run), :] = (
                past[0] * start_cell + past[1] * start_hidden + past[2]
            )
        rows = pl.ds(pl.multiple_of(block * LANES, LANES), LANES)
        out_ref[rows, :] = hidden_v[...].T

    @pl.when(my_tm < tm - 1)
    def _():
        pl.semaphore_wait(ready_sem, tm - 1 - my_tm)

    def scan_step(turn, carry):
        @pl.when(turn < blocks)
        def _():
            first(turn)

        @pl.when((turn >= 1) & (turn <= blocks))
        def _():
            second(turn - 1)

        @pl.when(turn >= 2)
        def _():
            third(turn - 2)

        return carry

    lax.fori_loop(0, blocks + 2, scan_step, 0)

    def settle_units(unit, carry):
        give_copy(unit).wait_send()

        @pl.when(unit < far)
        def _():
            far_copy(unit).wait_send()

        return carry

    lax.fori_loop(0, units, settle_units, 0)

    def settle_maps(index, carry):
        def settle(target, carry):
            map_copy(index // blocks, index % blocks, my_tm, target).wait_send()
            return carry

        return lax.fori_loop(my_tm + 1, tm, settle, carry)

    lax.fori_loop(0, 2 * blocks, settle_maps, 0)


def shards(chan, tm, tokens, in_weight, recur_weight, gate_bias, forget_offset):
    steps, depth = tokens.shape
    channels = recur_weight.shape[0]
    chips = chan // 2
    blocks = channels // LANES
    held = blocks * PIECES
    units = chips * held
    far = max(1, units - held)
    width = GATES * LANES
    thin = width // PIECES
    run = steps // SUB
    most = max(2.0 * KNEE, 2 * depth * TOKEN_MOST * WEIGHT_MOST)
    hbm = pl.BlockSpec(memory_space=pltpu.HBM)
    dma = pltpu.SemaphoreType.DMA
    float32 = jnp.float32
    return pl.pallas_call(
        functools.partial(kernel, chips, blocks, tm, most),
        out_shape=pltpu.VMEM((channels, steps), float32),
        in_specs=[hbm] * 5,
        out_specs=pl.BlockSpec(memory_space=pltpu.VMEM),
        scratch_shapes=[
            pltpu.VMEM((steps, depth), tokens.dtype),
            pltpu.VMEM((steps, depth), tokens.dtype),
            pltpu.VMEM((2 * units, depth, thin), in_weight.dtype),
            pltpu.VMEM((2, channels), float32),
            pltpu.VMEM((GATES, channels), float32),
            pltpu.VMEM((1, steps), float32),
            pltpu.VMEM((units, 2, steps, thin), float32),
            pltpu.VMEM((units, steps, thin), float32),
            pltpu.VMEM((far, steps, thin), jnp.bfloat16),
            pltpu.VMEM((far, steps, thin), jnp.bfloat16),
            pltpu.VMEM((width, width), jnp.bfloat16),
            pltpu.VMEM((max(1, chips - 1), GATES, steps, LANES), float32),
            pltpu.VMEM((width, steps), float32),
            pltpu.VMEM((blocks, GATES, steps, LANES), float32),
            pltpu.VMEM((blocks, 2, run, SUB, LANES), float32),
            pltpu.VMEM((blocks, run, SUB, LANES), float32),
            pltpu.VMEM((blocks, 8, run, SUB, LANES), float32),
            pltpu.VMEM((2, blocks, 6, SUB, LANES), float32),
            pltpu.VMEM((2 * blocks * tm, SUB, LANES), float32),
            pltpu.VMEM((steps, LANES), float32),
            dma,
            dma((3,)),
            dma((2 * units,)),
            dma((units,)),
            dma((units,)),
            dma((far,)),
            dma((far,)),
            dma((2 * blocks * tm,)),
            dma((2 * blocks * tm,)),
            pltpu.SemaphoreType.REGULAR,
        ],
        compiler_params=pltpu.CompilerParams(
            collective_id=0, has_side_effects=True, vmem_limit_bytes=65000 * 1024
        ),
    )(tokens, in_weight, recur_weight.T, gate_bias.T, forget_offset.reshape(1, steps))


def solution(mesh):
    placed = (
        P(("groups", "tm"), "chan"),
        P("chan", None),
        P("chan", None),
        P("chan", None),
        P(("groups", "tm")),
    )
    return jax.shard_map(
        functools.partial(shards, mesh.shape["chan"], mesh.shape["tm"]),
        mesh=mesh,
        in_specs=placed,
        out_specs=P("chan", ("groups", "tm")),
        check_vma=False,
    )
```

time: 47.5 us -> 23.3 us (0.49)
  the two profiles are of different devices: /device:TPU:0 before, /device:TPU:28 now
where the time goes in v1:
time: 23.3 us; the launch traced here: 23.2 us
  Pallas kernels  22.5 us (97%)
  local copies, waits for them, and re-layouts  0.71 us (3%)
    pallas_call x1, Pallas kernels, shards(): pl.pallas_call(functools.partial(kernel, chips, blocks, tm, most), out_sh...  22.5 us
    unnamed x1, local copies, waits for them, and re-layouts  0.71 us

profile of v1, /device:TPU:28, one launch (start us, length us, event | category | flops | bytes accessed | tf_op | source)
XLA Modules:
  0.0 23.2 jit_solution(9354445478687146206)
XLA Ops:
  0.0 22.5 %shard_map.55 = f32[512,128]{1,0:T(8,128)S(1)} custom-call(bf16[128,1024]{1,0:T(8,128)(2,1)} %tokens_hbm.1, bf16[1024,8192]{1,0:T(8,128)(2,1)} %weight_hbm.1, f32[2,512]{1,0:T(2,128)} %bitcast.4, f32[4,512]{1,0:T(4,128)} %bitcast.3, f32[1,128]{1,0:T(1,128)} %bitcast.5), custom_call_target="tpu_custom_call" | custom-call | tf_op jit(solution)/shard_map/pallas_call | solution.py:452
  22.5 0.7 %copy.7 = f32[512,128]{1,0:T(8,128)} copy(f32[512,128]{1,0:T(8,128)S(1)} %shard_map.55) | data formatting | bytes 524288
